TPU v7x, 32 devices: a whole 2x2x4 slice. The times are simulated.
32 devices in a mesh: grp: 4 (over y, x), grid: 8 (over z, core).
Axes of the slice: x: 2, y: 2, z: 4, core: 2. Of those that a mesh axis runs over, the one named last changes fastest.
Arguments:
- orbitals: float32 [64, 262144], P('grp', 'grid'), may hold values from -6 to 6
- anchors: int32 [64, 3], replicated, may hold values from 0 to 31
- pair_slots: int32 [32, 4, 2], replicated, may hold values from -1 to 63, as said below
Outputs:
- exchange_term: float32 [64, 262144], P('grp', 'grid')
Inputs may be any that keep to these rules, and one draw needn't show every extreme that they name: `pair_slots`: row k lists the pairs of owner k, the device with index k in the order grp, grid; its first slots hold pairs of two different orbital numbers and its other slots hold -1 in both columns. Exactly 64 slots hold pairs in all, no row holds more than 4, and some row holds exactly 4.
All inputs are finite; a program needn't handle non-finite values.
Results may differ from a plain program's by a relative error of at most 0.0003.
Values sent between devices are 32-bit elements; how exact they have to be, the bound alone decides.
A program may use at most 128 MiB of HBM per device.

v0:
```python
import jax
import jax.numpy as jnp
from jax import lax
from jax.sharding import PartitionSpec as P

B = 64
PAIR_DEV = 2
ITERS = 3


def shift_field(field, offset, extent):
    plane_size = extent * extent
    padded_x = jnp.pad(field, ((extent, extent), (0, 0)))
    moved = lax.dynamic_slice_in_dim(padded_x, extent - offset[0], extent, 0)
    padded_yz = jnp.pad(moved, ((0, 0), (plane_size, plane_size)))
    linear = offset[1] * extent + offset[2]
    moved = lax.dynamic_slice_in_dim(padded_yz, plane_size - linear, plane_size, 1)
    cells = lax.broadcasted_iota(jnp.int32, (1, plane_size), 1)
    coord_y = cells // extent - offset[1]
    coord_z = cells % extent - offset[2]
    inside = (coord_y >= 0) & (coord_y < extent) & (coord_z >= 0) & (coord_z < extent)
    return jnp.where(inside, moved, jnp.zeros_like(moved))


def operate(field, extent):
    padded_x = jnp.pad(field, ((1, 1), (0, 0)))
    beside = padded_x[2:] + padded_x[:-2]
    padded_y = jnp.pad(field, ((0, 0), (extent, extent)))
    beside = beside + padded_y[:, 2 * extent :] + padded_y[:, : -2 * extent]
    padded_z = jnp.pad(field, ((0, 0), (1, 1)))
    cells = lax.broadcasted_iota(jnp.int32, (1, field.shape[1]), 1) % extent
    upper_z = jnp.where(cells < extent - 1, padded_z[:, 2:], jnp.zeros_like(field))
    lower_z = jnp.where(cells > 0, padded_z[:, :-2], jnp.zeros_like(field))
    return 6.0 * field - beside - upper_z - lower_z


def conjugate(density, extent):
    potential = jnp.zeros_like(density)
    resid = density
    direction = density
    norm_now = jnp.sum(resid * resid)
    for turn in range(ITERS):
        image = operate(direction, extent)
        step_len = norm_now / jnp.sum(direction * image)
        potential = potential + step_len * direction
        resid = resid - step_len * image
        norm_next = jnp.sum(resid * resid)
        direction = resid + norm_next / norm_now * direction
        norm_now = norm_next
    return potential


def pair_terms(field_a, field_b, offset, extent):
    partner = shift_field(field_b, offset, extent)
    density = field_a * partner
    potential = conjugate(density, extent)
    term_a = potential * partner
    term_b = shift_field(potential * field_a, -offset, extent)
    return (term_a, term_b)


def deal_evenly(pair_slots, owner_count, each_owner):
    flat_slots = pair_slots.reshape(-1, 2)
    filled = (flat_slots[:, 0] >= 0).astype(jnp.int32)
    position = jnp.cumsum(filled, dtype=jnp.int32) - filled
    wanted = lax.broadcasted_iota(jnp.int32, (owner_count, each_owner), 1) * owner_count
    wanted = (wanted + lax.broadcasted_iota(jnp.int32, (owner_count, each_owner), 0)).reshape(-1)
    matched = (position[None, :] == wanted[:, None]) & (filled[None, :] == 1)
    picked = jnp.dot(matched.astype(jnp.int32), flat_slots)
    return picked.reshape(owner_count, each_owner, 2)


def body(orbitals, anchors, pair_slots):
    extent = B
    grid_count = lax.axis_size("grid")
    owner_count = lax.axis_size("grp") * grid_count
    group_idx = lax.axis_index("grp")
    place_idx = lax.axis_index("grid")
    assignment = deal_evenly(pair_slots, owner_count, PAIR_DEV)
    slot_count = assignment.shape[1]
    filled = assignment[..., 0] >= 0
    safe_ids = jnp.maximum(assignment, 0)
    pieces = lax.all_gather(orbitals, "grp", axis=0, tiled=True)
    group_table = lax.dynamic_slice_in_dim(safe_ids, group_idx * grid_count, grid_count, 0)
    gather_ids = jnp.transpose(group_table, (1, 2, 0))
    outgoing = pieces[gather_ids]
    arrived = lax.all_to_all(outgoing, "grid", split_axis=2, concat_axis=2, tiled=True)
    boxes = arrived.reshape(slot_count, 2, extent, extent * extent)
    owner_idx = group_idx * grid_count + place_idx
    own_pairs = safe_ids[owner_idx]
    own_filled = filled[owner_idx]
    offsets = anchors[own_pairs[:, 1]] - anchors[own_pairs[:, 0]]

    def solve_slot(slot_item):
        boxes_pair, offset, flag = slot_item
        term_a, term_b = pair_terms(boxes_pair[0], boxes_pair[1], offset, extent)
        weight_flag = jnp.where(flag, 1.0, 0.0).astype(jnp.float32)
        return jnp.stack([term_a, term_b]) * weight_flag

    terms = lax.map(solve_slot, (boxes, offsets, own_filled))
    returned = lax.all_to_all(
        terms.reshape(slot_count, 2, grid_count, -1),
        "grid",
        split_axis=2,
        concat_axis=2,
        tiled=True,
    )
    flat_terms = returned.reshape(-1, returned.shape[-1])
    summed = jax.ops.segment_sum(flat_terms, gather_ids.reshape(-1), num_segments=anchors.shape[0])
    return lax.psum_scatter(summed, "grp", scatter_dimension=0, tiled=True)


def solution(mesh):
    return jax.shard_map(
        body,
        mesh=mesh,
        in_specs=(P("grp", "grid"), P(), P()),
        out_specs=P("grp", "grid"),
        check_vma=False,
    )
```

profile of v0, /device:TPU:0, one launch (start us, length us, event | category | flops | bytes accessed | tf_op | source)
XLA Modules:
  0.0 509.3 jit_solution(14262574383303529083)
XLA Ops:
  6.5 0.7 all-gather.2.cloned.1.call-update
  7.3 0.8 copy.17
  8.2 0.2 reduce-window.8
  8.5 0.3 broadcast_maximum_fusion
  9.0 90.4 %all-gather.2.cloned.1.call-done = f32[64,32768]{1,0:T(8,128)} async-done(((f32[16,32768]{1,0:T(8,128)}), f32[64,32768]{1,0:T(8,128)}) %all-gather.2.cloned.1.call-update) | async-done | bytes 8388624 | tf_op jit(solution)/shard_map/all_gather | solution.py:83
  99.4 8.8 %gather_fusion = f32[32,32768]{1,0:T(8,128)} fusion(f32[64,32768]{1,0:T(8,128)} %all-gather.2.cloned.1.call-done, s32[1024]{0:T(1024)S(1)} %pad_clamp_fusion.2), kind=kCustom, calls=%fused_computation | custom fusion | bytes 8388736 | tf_op jit(solution)/shard_map/gather | solution.py:86
  108.2 7.4 %copy.19 = f32[2,2,8,32768]{3,1,0,2:T(2,128)} copy(f32[2,2,8,32768]{3,2,1,0:T(8,128)} %bitcast.60) | data formatting | bytes 8388608 | tf_op jit(solution)/shard_map/gather | solution.py:86
  115.6 4.9 all-to-all-start
  120.6 0.2 dynamic-slice_reduce_fusion
  120.8 0.2 fusion.63
  121.0 0.6 gather_fusion.2
  121.6 0.6 gather_fusion.1
  122.1 0.2 compare_reduce_fusion.1
  122.3 92.1 %all-to-all-done = f32[2,2,8,32768]{3,1,0,2:T(2,128)} async-done(((f32[2,2,8,32768]{3,1,0,2:T(2,128)}), f32[2,2,8,32768]{3,1,0,2:T(2,128)}, u32[]{:S(2)}, u32[]{:S(2)}) %all-to-all-start) | async-done | bytes 4194336 | tf_op jit(solution)/shard_map/all_to_all | solution.py:87
  214.4 6.6 %copy.20 = f32[2,2,8,32768]{3,2,1,0:T(8,128)} copy(f32[2,2,8,32768]{3,1,0,2:T(2,128)} %all-to-all-done) | data formatting | bytes 8388608 | tf_op jit(solution)/shard_map/all_to_all | solution.py:87
  221.0 4.9 reshape.254
  226.0 64.2 %while.13 = (s32[]{:T(128)}, f32[2,2,64,4096]{3,2,1,0:T(8,128)}, f32[2,2,64,4096]{3,2,1,0:T(8,128)}, s32[2,3]{1,0:T(2,128)S(1)}, pred[2]{0:T(512)(128)(4,1)S(1)}...) while((s32[]{:T(128)}, f32[2,2,64,4096]{3,2,1,0:T(8,128)}, ...), condition=%wide.region_8.9_spmd, body=%wide.region_1.8_spmd.sunk | while | flops 22224920 | bytes 80794384 | solution.py:100
  226.0 0.6 dynamic_slice.96
  227.2 0.6 fusion.80
  232.8 1.2 fusion.85
  234.0 1.2 fusion.81
  235.3 1.3 dynamic-slice_bitcast_fusion.5
  236.6 0.1 pad_dynamic-slice_fusion.6
  236.7 1.0 copy-done
  237.7 1.6 fusion.82
  239.3 1.8 multiply_reduce_fusion.9
  242.3 0.9 multiply_reduce_fusion.10
  244.4 0.1 multiply_add_fusion.5
  244.5 1.8 multiply_reduce_fusion.11
  247.6 0.9 multiply_reduce_fusion.12
  249.7 0.3 multiply_add_fusion.6
  250.0 1.8 fusion.84
  253.0 2.3 multiply_bitcast_fusion.2
  255.3 0.1 pad_dynamic-slice_fusion.7
  255.4 0.3 fusion.86
  255.8 0.2 fusion.87
  256.0 2.0 copy-done.2
  258.0 0.6 dynamic_slice.96
  259.3 0.6 fusion.80
  264.9 1.2 fusion.85
  266.1 1.2 fusion.81
  267.3 1.3 dynamic-slice_bitcast_fusion.5
  268.6 0.1 pad_dynamic-slice_fusion.6
  268.8 1.0 copy-done
  269.7 1.6 fusion.82
  271.3 1.8 multiply_reduce_fusion.9
  274.4 0.9 multiply_reduce_fusion.10
  276.5 0.1 multiply_add_fusion.5
  276.6 1.8 multiply_reduce_fusion.11
  279.7 0.9 multiply_reduce_fusion.12
  281.8 0.3 multiply_add_fusion.6
  282.1 1.8 fusion.84
  285.1 2.3 multiply_bitcast_fusion.2
  287.4 0.1 pad_dynamic-slice_fusion.7
  287.6 0.3 fusion.86
  288.0 0.2 fusion.87
  288.2 2.0 copy-done.2
  290.2 4.9 reshape.255
  295.1 7.4 %copy.23 = f32[2,2,8,32768]{3,1,0,2:T(2,128)} copy(f32[2,2,8,32768]{3,2,1,0:T(8,128)} %reshape.255) | data formatting | bytes 8388608 | tf_op jit(solution)/shard_map/reshape | solution.py:102
  302.5 4.5 all-to-all-start.1
  307.2 93.8 %all-to-all-done.1 = f32[2,2,8,32768]{3,1,0,2:T(2,128)} async-done(((f32[2,2,8,32768]{3,1,0,2:T(2,128)}), f32[2,2,8,32768]{3,1,0,2:T(2,128)}, u32[]{:S(2)}, u32[]{:S(2)}) %all-to-all-start.1) | async-done | bytes 4194336 | tf_op jit(solution)/shard_map/all_to_all | solution.py:101
  401.0 6.6 %copy.24 = f32[2,2,8,32768]{3,2,1,0:T(8,128)} copy(f32[2,2,8,32768]{3,1,0,2:T(2,128)} %all-to-all-done.1) | data formatting | bytes 8388608 | tf_op jit(solution)/shard_map/all_to_all | solution.py:101
  407.6 10.4 %scatter_custom_fusion = f32[64,32768]{1,0:T(8,128)} fusion(s32[32]{0:T(128)S(1)} %reshape.283, f32[32,32768]{1,0:T(8,128)} %bitcast.61, f32[]{:T(128)} %constant.162.clone.1), kind=kCustom, calls=%fused_computation.86 | custom fusion | flops 1048576 | bytes 8389120 | tf_op jit(solution)/shard_map/scatter-add | solution.py:109
  418.0 84.4 %reduce-scatter.2.cloned.1.call-done = f32[16,32768]{1,0:T(8,128)} async-done(((f32[64,32768]{1,0:T(8,128)}), f32[16,32768]{1,0:T(8,128)}) %reduce-scatter.2.cloned.1.call-update) | async-done | bytes 2097168 | tf_op jit(solution)/shard_map/reduce_scatter | solution.py:110
  (30 shorter events, 0.8 us)
Async XLA Ops:
  6.5 92.9 %all-gather.2.cloned.1.call-start = ((), (), s32[]{:S(2)}) async-start(), calls=%async_computation.3 | async-start | bytes 10485760 | tf_op jit(solution)/shard_map/all_gather | solution.py:83
  115.6 4.9 copy-start.3
  115.6 98.8 %all-to-all-start = ((f32[2,2,8,32768]{3,1,0,2:T(2,128)}), f32[2,2,8,32768]{3,1,0,2:T(2,128)}, u32[]{:S(2)}, u32[]{:S(2)}) async-start(f32[2,2,8,32768]{3,1,0,2:T(2,128)} %copy.19), calls=%async_computation | async-start | bytes 8388608 | tf_op jit(solution)/shard_map/all_to_all | solution.py:87
  236.7 1.0 copy-start
  253.0 2.8 copy-start.1
  256.0 2.0 copy-start.2
  268.8 1.0 copy-start
  285.1 2.8 copy-start.1
  288.2 2.0 copy-start.2
  302.5 98.5 %all-to-all-start.1 = ((f32[2,2,8,32768]{3,1,0,2:T(2,128)}), f32[2,2,8,32768]{3,1,0,2:T(2,128)}, u32[]{:S(2)}, u32[]{:S(2)}) async-start(f32[2,2,8,32768]{3,1,0,2:T(2,128)} %copy.23), calls=%async_computation.1 | async-start | bytes 8388608 | tf_op jit(solution)/shard_map/all_to_all | solution.py:101
  307.0 195.4 %reduce-scatter.2.cloned.1.call-start = ((), (), s32[]{:S(2)}) async-start(), calls=%async_computation.4 | async-start | bytes 10485760 | tf_op jit(solution)/shard_map/reduce_scatter | solution.py:110
Sparse Core Ops, SparseCore 0:
  9.2 90.1 all-gather.1
  418.1 84.2 reduce-scatter.1
where the time goes:
time: 511 us; the launch traced here: 509 us
  waiting for transfers between devices  362 us (71%)
  local copies, waits for them, and re-layouts  60.4 us (12%)
  other arithmetic  40.1 us (8%)
  loops' own time  24.1 us (5%)
  between operations  13.5 us (3%)
  starting transfers between devices  9.44 us (2%)
    all_to_all x1, waiting for transfers between devices, body(): lax.all_to_all(terms.reshape(slot_count, 2, grid_count, -1), 'grid', spli...  93.8 us
    all_to_all x1, waiting for transfers between devices, body(): lax.all_to_all(outgoing, 'grid', split_axis=2, concat_axis=2, tiled=True)  92.1 us
    all_gather x1, waiting for transfers between devices, body(): pieces = lax.all_gather(orbitals, 'grp', axis=0, tiled=True)  90.4 us
    reduce_scatter x1, waiting for transfers between devices, body(): return lax.psum_scatter(summed, 'grp', scatter_dimension=0, tiled=True)  84.4 us
    another operation x1, loops' own time, body(): terms = lax.map(solve_slot, (boxes, offsets, own_filled))  24.1 us
    gather x2, local copies, waits for them, and re-layouts, body(): outgoing = pieces[gather_ids]  16.2 us
    reshape x2, local copies, waits for them, and re-layouts, body(): terms.reshape(slot_count, 2, grid_count, -1)  12.3 us
    reduce_sum x6, other arithmetic, conjugate(): step_len = norm_now / jnp.sum(direction * image)  10.6 us
  transfers between devices with their start and end apart: 4, of which 4 were waited for; matrix products, arithmetic and copies ran while one was open for 1% of the time, Pallas kernels for 0%

commit v1 on v0

--- a/solution.py
+++ b/solution.py
@@ -98,12 +98,18 @@
         return jnp.stack([term_a, term_b]) * weight_flag
 
     terms = lax.map(solve_slot, (boxes, offsets, own_filled))
-    returned = lax.all_to_all(
-        terms.reshape(slot_count, 2, grid_count, -1),
-        "grid",
-        split_axis=2,
-        concat_axis=2,
-        tiled=True,
+    returned = jnp.concatenate(
+        lax.all_to_all(
+            jnp.stack(
+                jnp.split(
+                    terms.reshape(slot_count, 2, grid_count, -1), lax.axis_size("grid"), axis=2
+                )
+            ),
+            "grid",
+            0,
+            0,
+        ),
+        axis=2,
     )
     flat_terms = returned.reshape(-1, returned.shape[-1])
     summed = jax.ops.segment_sum(flat_terms, gather_ids.reshape(-1), num_segments=anchors.shape[0])

time: 511 us -> 531 us (1.039)
  local copies, waits for them, and re-layouts: 60.4 us -> 80.4 us
    unnamed x4 -> x11, local copies, waits for them, and re-layouts: 0.89 us -> 24.8 us
    reshape x2 -> x1, local copies, waits for them, and re-layouts: 12.3 us -> 4.97 us  [body(): terms.reshape(slot_count, 2, grid_count, -1)]
    all_to_all x1 -> x0, local copies, waits for them, and re-layouts: 6.59 us -> none  [body(): lax.all_to_all(terms.reshape(slot_count, 2, grid_count, -1), 'grid', spli...]
    reshape x0 -> x1, local copies, waits for them, and re-layouts: none -> 6.54 us  [body(): jnp.concatenate(lax.all_to_all(jnp.stack(jnp.split(terms.reshape(slot_cou...]
where the time goes in v1:
time: 531 us; the launch traced here: 529 us
  waiting for transfers between devices  362 us (68%)
  local copies, waits for them, and re-layouts  80.4 us (15%)
  other arithmetic  40.3 us (8%)
  loops' own time  23.9 us (5%)
  between operations  13.5 us (3%)
  starting transfers between devices  9.45 us (2%)
    all_to_all x1, waiting for transfers between devices, body(): lax.all_to_all(jnp.stack(jnp.split(terms.reshape(slot_count, 2, grid_coun...  93.8 us
    all_to_all x1, waiting for transfers between devices, body(): lax.all_to_all(outgoing, 'grid', split_axis=2, concat_axis=2, tiled=True)  92.1 us
    all_gather x1, waiting for transfers between devices, body(): pieces = lax.all_gather(orbitals, 'grp', axis=0, tiled=True)  90.4 us
    reduce_scatter x1, waiting for transfers between devices, body(): return lax.psum_scatter(summed, 'grp', scatter_dimension=0, tiled=True)  84.4 us
    unnamed x11, local copies, waits for them, and re-layouts  24.8 us
    another operation x1, loops' own time, body(): terms = lax.map(solve_slot, (boxes, offsets, own_filled))  23.9 us
    gather x2, local copies, waits for them, and re-layouts, body(): outgoing = pieces[gather_ids]  16.2 us
  transfers between devices with their start and end apart: 4, of which 4 were waited for; matrix products, arithmetic and copies ran while one was open for 1% of the time, Pallas kernels for 0%

profile of v1, /device:TPU:0, one launch (start us, length us, event | category | flops | bytes accessed | tf_op | source)
XLA Modules:
  0.0 529.2 jit_solution(410441295305555252)
XLA Ops:
  6.5 0.7 all-gather.2.cloned.1.call-update
  7.3 0.8 copy.26
  8.5 0.3 broadcast_maximum_fusion
  9.0 90.4 %all-gather.2.cloned.1.call-done = f32[64,32768]{1,0:T(8,128)} async-done(((f32[16,32768]{1,0:T(8,128)}), f32[64,32768]{1,0:T(8,128)}) %all-gather.2.cloned.1.call-update) | async-done | bytes 8388624 | tf_op jit(solution)/shard_map/all_gather | solution.py:83
  99.4 8.8 %gather_fusion = f32[32,32768]{1,0:T(8,128)} fusion(f32[64,32768]{1,0:T(8,128)} %all-gather.2.cloned.1.call-done, s32[1024]{0:T(1024)S(1)} %pad_clamp_fusion.2), kind=kCustom, calls=%fused_computation | custom fusion | bytes 8388736 | tf_op jit(solution)/shard_map/gather | solution.py:86
  108.2 7.4 %copy.28 = f32[2,2,8,32768]{3,1,0,2:T(2,128)} copy(f32[2,2,8,32768]{3,2,1,0:T(8,128)} %bitcast.93) | data formatting | bytes 8388608 | tf_op jit(solution)/shard_map/gather | solution.py:86
  115.6 4.9 all-to-all-start
  120.6 0.2 dynamic-slice_reduce_fusion
  120.8 0.2 fusion.71
  121.0 0.6 gather_fusion.2
  121.5 0.6 gather_fusion.1
  122.1 0.2 compare_reduce_fusion.1
  122.3 92.1 %all-to-all-done = f32[2,2,8,32768]{3,1,0,2:T(2,128)} async-done(((f32[2,2,8,32768]{3,1,0,2:T(2,128)}), f32[2,2,8,32768]{3,1,0,2:T(2,128)}, u32[]{:S(2)}, u32[]{:S(2)}) %all-to-all-start) | async-done | bytes 4194336 | tf_op jit(solution)/shard_map/all_to_all | solution.py:87
  214.4 6.6 %copy.29 = f32[2,2,8,32768]{3,2,1,0:T(8,128)} copy(f32[2,2,8,32768]{3,1,0,2:T(2,128)} %all-to-all-done) | data formatting | bytes 8388608 | tf_op jit(solution)/shard_map/all_to_all | solution.py:87
  221.0 5.0 reshape.254
  225.9 64.2 %while.13 = (s32[]{:T(128)}, f32[2,2,64,4096]{3,2,1,0:T(8,128)}, f32[2,2,64,4096]{3,2,1,0:T(8,128)}, s32[2,3]{1,0:T(2,128)S(1)}, pred[2]{0:T(512)(128)(4,1)S(1)}...) while((s32[]{:T(128)}, f32[2,2,64,4096]{3,2,1,0:T(8,128)}, ...), condition=%wide.region_8.9_spmd, body=%wide.region_1.8_spmd.sunk | while | flops 22224920 | bytes 80794384 | solution.py:100
  225.9 0.6 dynamic_slice.96
  227.2 0.7 fusion.88
  232.8 1.2 fusion.93
  234.1 1.2 fusion.89
  235.3 1.3 dynamic-slice_bitcast_fusion.5
  236.8 1.0 copy-done
  237.7 1.6 fusion.90
  239.3 1.8 multiply_reduce_fusion.9
  242.3 0.9 multiply_reduce_fusion.10
  244.6 1.8 multiply_reduce_fusion.11
  247.6 0.9 multiply_reduce_fusion.12
  249.8 0.3 multiply_add_fusion.6
  250.0 1.8 fusion.92
  253.0 2.3 multiply_bitcast_fusion.2
  255.4 0.3 fusion.94
  255.8 0.2 fusion.95
  256.1 1.9 copy-done.2
  258.0 0.6 dynamic_slice.96
  259.2 0.7 fusion.88
  264.9 1.2 fusion.93
  266.1 1.2 fusion.89
  267.3 1.3 dynamic-slice_bitcast_fusion.5
  268.8 1.0 copy-done
  269.8 1.6 fusion.90
  271.4 1.8 multiply_reduce_fusion.9
  274.4 0.9 multiply_reduce_fusion.10
  276.6 1.8 multiply_reduce_fusion.11
  279.7 0.9 multiply_reduce_fusion.12
  281.8 0.3 multiply_add_fusion.6
  282.1 1.8 fusion.92
  285.1 2.3 multiply_bitcast_fusion.2
  287.6 0.3 fusion.94
  287.9 0.2 fusion.95
  288.2 1.9 copy-done.2
  290.1 5.0 reshape.255
  295.1 3.2 fusion.62
  298.3 3.4 fusion.61
  301.8 3.5 fusion.60
  305.2 3.4 fusion.59
  308.7 3.4 fusion.58
  312.1 3.4 fusion.57
  315.6 3.4 fusion.56
  319.0 3.4 fusion.55
  322.4 4.5 all-to-all-start.1
  327.1 93.8 %all-to-all-done.1 = f32[8,2,2,1,32768]{4,3,2,1,0:T(1,128)} async-done(((f32[8,2,2,1,32768]{4,3,2,1,0:T(1,128)}), f32[8,2,2,1,32768]{4,3,2,1,0:T(1,128)}, u32[]{:S(2)}, u32[]{:S(2)}) %all-to-all-start.1) | async-done | bytes 4194336 | tf_op jit(solution)/shard_map/all_to_all | solution.py:102
  421.0 6.5 %copy.32 = f32[2,2,8,1,32768]{4,2,1,0,3:T(8,128)} copy(f32[2,2,8,1,32768]{4,3,1,0,2:T(1,128)} %bitcast.25) | data formatting | bytes 8388608 | tf_op jit(solution)/shard_map/reshape | solution.py:101
  427.5 10.4 %scatter_custom_fusion = f32[64,32768]{1,0:T(8,128)} fusion(s32[32]{0:T(128)S(1)} %reshape.283, f32[32,32768]{1,0:T(8,128)} %bitcast.94, f32[]{:T(128)} %constant.162.clone.1), kind=kCustom, calls=%fused_computation.86 | custom fusion | flops 1048576 | bytes 8389120 | tf_op jit(solution)/shard_map/scatter-add | solution.py:115
  438.0 84.4 %reduce-scatter.2.cloned.1.call-done = f32[16,32768]{1,0:T(8,128)} async-done(((f32[64,32768]{1,0:T(8,128)}), f32[16,32768]{1,0:T(8,128)}) %reduce-scatter.2.cloned.1.call-update) | async-done | bytes 2097168 | tf_op jit(solution)/shard_map/reduce_scatter | solution.py:116
  (37 shorter events, 1.8 us)
Async XLA Ops:
  6.5 92.9 %all-gather.2.cloned.1.call-start = ((), (), s32[]{:S(2)}) async-start(), calls=%async_computation.3 | async-start | bytes 10485760 | tf_op jit(solution)/shard_map/all_gather | solution.py:83
  115.6 4.9 copy-start.3
  115.6 98.8 %all-to-all-start = ((f32[2,2,8,32768]{3,1,0,2:T(2,128)}), f32[2,2,8,32768]{3,1,0,2:T(2,128)}, u32[]{:S(2)}, u32[]{:S(2)}) async-start(f32[2,2,8,32768]{3,1,0,2:T(2,128)} %copy.28), calls=%async_computation | async-start | bytes 8388608 | tf_op jit(solution)/shard_map/all_to_all | solution.py:87
  236.7 1.0 copy-start
  253.0 2.8 copy-start.1
  256.0 1.9 copy-start.2
  268.8 1.0 copy-start
  285.1 2.8 copy-start.1
  288.2 1.9 copy-start.2
  322.4 98.5 %all-to-all-start.1 = ((f32[8,2,2,1,32768]{4,3,2,1,0:T(1,128)}), f32[8,2,2,1,32768]{4,3,2,1,0:T(1,128)}, u32[]{:S(2)}, u32[]{:S(2)}) async-start(f32[8,2,2,1,32768]{4,3,2,1,0:T(1,128)} %fusion.55), calls=%async_computation.1 | async-start | bytes 8388608 | tf_op jit(solution)/shard_map/all_to_all | solution.py:102
  327.0 195.4 %reduce-scatter.2.cloned.1.call-start = ((), (), s32[]{:S(2)}) async-start(), calls=%async_computation.4 | async-start | bytes 10485760 | tf_op jit(solution)/shard_map/reduce_scatter | solution.py:116
Sparse Core Ops, SparseCore 0:
  9.2 90.1 all-gather.1
  438.1 84.2 reduce-scatter.1
